TPU v7x, 32 devices: a whole 2x2x4 slice. The times are simulated.
32 devices in a mesh: section: 2 (over x), expert: 4 (over z), tensor: 4 (over y, core).
Axes of the slice: x: 2, y: 2, z: 4, core: 2. Of those that a mesh axis runs over, the one named last changes fastest.
Arguments:
- layer_inputs: bfloat16 [2, 2, 320, 3072], P('section', None, 'expert', 'tensor'), may hold values from -6 to 6
- grad_out: bfloat16 [2, 320, 3072], P(None, 'expert', 'tensor'), may hold values from -6 to 6
- norm_gain: bfloat16 [2, 3072], P('section', 'tensor'), may hold values from 0.25 to 1.75
- router_w: bfloat16 [2, 3072, 4], P('section', 'tensor'), may hold values from -0.21875 to 0.21875
- w_gate: bfloat16 [2, 3072, 32768], P('section', None, ('expert', 'tensor')), may hold values from -0.109375 to 0.109375
- w_up: bfloat16 [2, 3072, 32768], P('section', None, ('expert', 'tensor')), may hold values from -0.109375 to 0.109375
- w_down: bfloat16 [2, 32768, 3072], P('section', ('expert', 'tensor')), may hold values from -0.0625 to 0.0625
- saved_gate: bfloat16 [2, 2, 4, 64, 32768], P('section', None, None, None, ('expert', 'tensor')), may hold values from -6 to 6
- saved_up: bfloat16 [2, 2, 4, 64, 32768], P('section', None, None, None, ('expert', 'tensor')), may hold values from -6 to 6
- routes: int32 [2, 2, 320, 2], P('section', None, 'expert'), may hold values from 0 to 3, all different within a row; in each aligned block of 80 rows (0 to 79, 80 to 159, ..., all dimensions but the last counted through in order) at most 64 rows name the same one
Outputs:
- layer_grads: bfloat16 [2, 2, 320, 3072], P('section', None, 'expert', 'tensor')
Inputs may be any that keep to these rules, and one draw needn't show every extreme that they name: `routes`: each token names two different experts; within the 80 tokens of one device's aligned block of a layer and micro-batch, no expert is named by more than 64 tokens, and in some blocks one expert is named by exactly 64.
All inputs are finite; a program needn't handle non-finite values.
Results may differ from a plain program's by a relative error of at most 0.011.
Values may be sent and summed in bfloat16 or wider, within the bound.
A program may use at most 128 MiB of HBM per device.

v0:
```python
import jax
import jax.numpy as jnp
from jax import lax
from jax.sharding import PartitionSpec as P

norm_eps = 1e-05
highest = lax.Precision.HIGHEST


def from_behind(block, axis, distance):
    devices = range(lax.axis_size(axis))
    route = [(i - distance, i) for i in devices if i - distance in devices]
    return lax.ppermute(block, axis, route)


def on_device(
    layer_inputs, grad_out, norm_gain, router_w, w_gate, w_up, w_down, saved_gate, saved_up, routes
):
    sections = lax.axis_size("section")
    position = lax.axis_index("section")
    holders = lax.axis_size("expert")
    micros = grad_out.shape[0]
    tokens_here = grad_out.shape[1]
    quarter = grad_out.shape[2]
    gain_full = norm_gain[0].astype(jnp.float32)
    router = router_w[0]
    gate_mat = w_gate[0]
    up_mat = w_up[0]
    down_mat = w_down[0]
    width_all = gate_mat.shape[0]
    experts = router.shape[1]
    group = holders // experts
    capacity = saved_gate.shape[3]
    slot_count = experts * capacity
    slot_ids = jnp.arange(slot_count, dtype=jnp.int32)
    expert_ids = jnp.arange(experts, dtype=jnp.int32)

    def add_columns(piece):
        return jnp.einsum("scw,fw->scf", piece, down_mat, preferred_element_type=jnp.float32)

    def layer_back(inputs, upstream, chosen, gate_saved, up_saved):
        values = inputs.astype(jnp.float32)
        squares = lax.psum(jnp.sum(values * values, axis=-1), "tensor")
        scale = lax.rsqrt(squares / width_all + norm_eps)[:, None]
        normed = (values * scale * gain_full).astype(jnp.bfloat16)
        partial_logits = jnp.dot(normed, router, preferred_element_type=jnp.float32)
        logits = lax.psum(partial_logits, "tensor")
        onehot = (chosen[:, :, None] == expert_ids[None, None, :]).astype(jnp.float32)
        picked = jnp.sum(onehot * logits[:, None, :], axis=-1)
        first = jax.nn.sigmoid(picked[:, 0] - picked[:, 1])
        second = jax.nn.sigmoid(picked[:, 1] - picked[:, 0])
        flat_hot = onehot.reshape(tokens_here * 2, experts)
        earlier = jnp.cumsum(flat_hot, axis=0) - flat_hot
        within = jnp.sum(earlier * flat_hot, axis=-1).astype(jnp.int32)
        target = chosen.reshape(tokens_here * 2) * capacity + within
        placing = (
            (slot_ids[:, None] == target[None, :])
            .astype(jnp.float32)
            .reshape(slot_count, tokens_here, 2)
        )
        select = jnp.sum(placing, axis=-1).astype(jnp.bfloat16)
        upstream_send = jnp.dot(select, upstream, preferred_element_type=jnp.float32).astype(
            jnp.bfloat16
        )
        copies = jnp.broadcast_to(
            upstream_send.reshape(experts, 1, capacity, quarter),
            (experts, group, capacity, quarter),
        ).reshape(holders, capacity, quarter)
        arrived = lax.all_to_all(copies, "expert", split_axis=0, concat_axis=0, tiled=True)
        back_act = add_columns(lax.all_gather(arrived, "tensor", axis=2, tiled=True))
        gate_act = gate_saved.astype(jnp.float32)
        up_act = up_saved.astype(jnp.float32)
        sigma = jax.nn.sigmoid(gate_act)
        swish = gate_act * sigma
        weight_part = jnp.sum(swish * up_act * back_act, axis=-1)
        slope = sigma * (1.0 + gate_act * (1.0 - sigma))
        gate_grad = (back_act * up_act * slope).astype(jnp.bfloat16)
        up_grad = (back_act * swish).astype(jnp.bfloat16)
        unit = jnp.einsum("scf,df->scd", gate_grad, gate_mat, preferred_element_type=jnp.float32)
        unit = unit + jnp.einsum("scf,df->scd", up_grad, up_mat, preferred_element_type=jnp.float32)
        weighted = placing[:, :, 0] * first[None, :] + placing[:, :, 1] * second[None, :]
        unit_share = lax.psum_scatter(unit, "tensor", scatter_dimension=2, tiled=True)
        back_units, back_weights = (
            lax.all_to_all(unit_share, "expert", split_axis=0, concat_axis=0, tiled=True),
            lax.all_to_all(weight_part, "expert", split_axis=0, concat_axis=0, tiled=True),
        )
        slot_units = jnp.sum(back_units.reshape(experts, group, capacity, quarter), axis=1).reshape(
            slot_count, quarter
        )
        slot_weight = jnp.sum(back_weights.reshape(experts, group, capacity), axis=1).reshape(
            slot_count
        )
        hidden_grad = lax.dot_general(
            weighted, slot_units, (((0,), (0,)), ((), ())), precision=highest
        )
        prob_part = jnp.einsum("stk,s->tk", placing, slot_weight, precision=highest)
        prob_grad = lax.psum(prob_part, "tensor")
        logit_step = first * second * (prob_grad[:, 0] - prob_grad[:, 1])
        logit_grad = (onehot[:, 0, :] - onehot[:, 1, :]) * logit_step[:, None]
        hidden_grad = hidden_grad + jnp.einsum(
            "te,de->td", logit_grad, router.astype(jnp.float32), precision=highest
        )
        gained = hidden_grad * gain_full
        moment = lax.psum(jnp.sum(values * gained, axis=-1), "tensor")[:, None] / width_all
        result = (
            upstream.astype(jnp.float32) + scale * gained - values * scale * scale * scale * moment
        )
        return result.astype(jnp.bfloat16)

    def advance(tick, carry):
        incoming, grads = carry
        micro_id = tick - (sections - 1 - position)
        valid = jnp.logical_and(micro_id >= 0, micro_id < micros)
        safe_id = jnp.clip(micro_id, 0, micros - 1)
        inputs = lax.dynamic_index_in_dim(layer_inputs[0], safe_id, 0, keepdims=False)
        top_grad = lax.dynamic_index_in_dim(grad_out, safe_id, 0, keepdims=False)
        chosen = lax.dynamic_index_in_dim(routes[0], safe_id, 0, keepdims=False)
        gate_saved = lax.dynamic_index_in_dim(saved_gate[0], safe_id, 0, keepdims=False)
        up_saved = lax.dynamic_index_in_dim(saved_up[0], safe_id, 0, keepdims=False)
        upstream = jnp.where(position == sections - 1, top_grad, incoming)
        computed = layer_back(inputs, upstream, chosen, gate_saved, up_saved)
        result = jnp.where(valid, computed, jnp.zeros_like(computed))
        updated = lax.dynamic_update_index_in_dim(grads, result, safe_id, 0)
        grads = jnp.where(valid, updated, grads)
        incoming = from_behind(result, "section", -1)
        return (incoming, grads)

    start = (
        jnp.zeros((tokens_here, quarter), jnp.bfloat16),
        jnp.zeros((micros, tokens_here, quarter), jnp.bfloat16),
    )
    final_in, grads = lax.fori_loop(0, micros + sections - 1, advance, start)
    return grads[None]


def solution(mesh):
    placed = (
        P("section", None, "expert", "tensor"),
        P(None, "expert", "tensor"),
        P("section", "tensor"),
        P("section", "tensor", None),
        P("section", None, ("expert", "tensor")),
        P("section", None, ("expert", "tensor")),
        P("section", ("expert", "tensor"), None),
        P("section", None, None, None, ("expert", "tensor")),
        P("section", None, None, None, ("expert", "tensor")),
        P("section", None, "expert", None),
    )
    return jax.shard_map(
        on_device,
        mesh=mesh,
        in_specs=placed,
        out_specs=P("section", None, "expert", "tensor"),
        check_vma=False,
    )
```

profile of v0, /device:TPU:0, one launch (start us, length us, event | category | flops | bytes accessed | tf_op | source)
XLA Modules:
  0.0 453.6 jit_solution(15014488951981677367)
XLA Ops:
  7.3 438.8 %while.19 = (s32[]{:T(128)}, bf16[80,768]{1,0:T(8,128)(2,1)S(1)}, bf16[2,80,768]{2,1,0:T(8,128)(2,1)S(1)}, s32[]{:T(128)}, pred[]{:T(512)}, /*index=5*/bf16[2,80...) while((s32[]{:T(128)}, bf16[80,768]{1,0:T(8,128)(2,1)S(1)}, ...), condition=%wide.region_14.15_spmd.clone.clone, body=%wide.region_0.14_spmd.clone.clone.sunk | while | flops 9905498112 | bytes 112821912 | solution.py:132
  12.3 17.9 %all_to_all.47 = bf16[4,64,768]{2,1,0:T(8,128)(2,1)} all-to-all(bf16[4,64,768]{2,1,0:T(8,128)(2,1)S(1)} %bitcast.166), channel_id=1, replica_groups=mesh['section'=2,'expert'=4,'tensor'=4] {'expert'}, dimensions={0} | all-to-all | bytes 786432 | tf_op jit(solution)/shard_map/while/body/eval_jaxpr/all_to_all | solution.py:69
  30.3 18.8 %all-gather.2.cloned.1.call-done = bf16[4,64,3072]{2,1,0:T(8,128)(2,1)} async-done(((bf16[4,64,768]{2,1,0:T(8,128)(2,1)}), bf16[4,64,3072]{2,1,0:T(8,128)(2,1)}) %all-gather.2.cloned.1.call-update) | async-done | bytes 1572880 | tf_op jit(solution)/shard_map/while/body/eval_jaxpr/all_gather | solution.py:70
  49.2 9.9 %fusion.123 = (f32[4,64]{1,0:T(4,128)}, f32[4,64,2048]{2,1,0:T(8,128)S(1)}) fusion(bf16[1,2,4,64,2048]{4,3,2,1,0:T(8,128)(2,1)S(1)} %copy-done.5, s32[]{:T(128)S(6)} %min.13, bf16[1,2,4,64,2048]{4,3,2,1,0:T(8,128)(2,1)} %get-tuple-element.699, bf16[4,64,3072]{2,1,0:T(8,128)(2,1)} %all-gather.2.cloned.1.call-done, ...), kind=kOutput, calls=%fused_computation.17.clone.1 | convolution fusion | flops 3225943808 | bytes 18351108 | tf_op jit(solution)/shard_map/while/body/eval_jaxpr/scw,fw->scf/dot_general | solution.py:39
  59.1 10.7 %fusion.129 = f32[4,64,3072]{2,1,0:T(8,128)} fusion(bf16[3072,2048]{1,0:T(8,128)(2,1)} %get-tuple-element.701, f32[4,64,2048]{2,1,0:T(8,128)S(1)} %get-tuple-element.640, bf16[1,2,4,64,2048]{4,3,2,1,0:T(8,128)(2,1)S(1)} %copy-done.6, s32[]{:T(128)S(6)} %min.13), kind=kOutput, calls=%fused_computation.2.clone.1 | convolution fusion | flops 3224895488 | bytes 18874372 | tf_op jit(solution)/shard_map/while/body/eval_jaxpr/scf,df->scd/dot_general | solution.py:80
  69.8 11.6 %fusion.130 = f32[4,64,3072]{2,1,0:T(8,128)} fusion(f32[4,64,3072]{2,1,0:T(8,128)} %fusion.129, bf16[3072,2048]{1,0:T(8,128)(2,1)} %get-tuple-element.700, f32[4,64,2048]{2,1,0:T(8,128)} %copy-done.7, bf16[1,2,4,64,2048]{4,3,2,1,0:T(8,128)(2,1)S(1)} %copy-done.6, s32[]{:T(128)S(6)} %min.13, bf16[1,2,4,64,2048]{4,3,2,1,0:T(8,128)(2,1)S(1)} %copy-done.5), kind=kOutput, calls=%fused_computation.8.clone.1 | convolution fusion | flops 3228303360 | bytes 23068676 | tf_op jit(solution)/shard_map/while/body/eval_jaxpr/scf,df->scd/dot_general | solution.py:79
  98.8 20.5 %reduce-scatter.2.cloned.1.call-done = f32[4,64,768]{2,1,0:T(8,128)} async-done(((f32[4,64,3072]{2,1,0:T(8,128)}), f32[4,64,768]{2,1,0:T(8,128)}) %reduce-scatter.2.cloned.1.call-update) | async-done | bytes 786448 | tf_op jit(solution)/shard_map/while/body/eval_jaxpr/reduce_scatter | solution.py:82
  125.5 6.1 %all-reduce.3 = (f32[80,2]{0,1:T(2,128)S(1)}, f32[80,4]{0,1:T(4,128)S(1)}) all-reduce(f32[80,2]{0,1:T(2,128)S(1)} %bitcast.172, f32[80,4]{0,1:T(4,128)S(1)} %fusion.126), channel_id=1, replica_groups=mesh['section'=2,'expert'=4,'tensor'=4] {'tensor'}, use_global_device_ids=true, to_apply=%region_11.11 | all-reduce | flops 480 | bytes 3840 | tf_op jit(solution)/shard_map/while/body/eval_jaxpr/psum | solution.py:97
  131.9 12.0 %all-to-all-done.2 = f32[4,64,768]{2,1,0:T(8,128)S(1)} async-done(((f32[4,64,768]{2,1,0:T(8,128)}), f32[4,64,768]{2,1,0:T(8,128)S(1)}, u32[]{:S(2)}, u32[]{:S(2)}) %all-to-all-start.2) | async-done | bytes 786464 | tf_op jit(solution)/shard_map/while/body/eval_jaxpr/all_to_all | solution.py:84
  162.5 13.6 %all_to_all.47 = bf16[4,64,768]{2,1,0:T(8,128)(2,1)} all-to-all(bf16[4,64,768]{2,1,0:T(8,128)(2,1)S(1)} %bitcast.166), channel_id=1, replica_groups=mesh['section'=2,'expert'=4,'tensor'=4] {'expert'}, dimensions={0} | all-to-all | bytes 786432 | tf_op jit(solution)/shard_map/while/body/eval_jaxpr/all_to_all | solution.py:69
  176.2 17.3 %all-gather.2.cloned.1.call-done = bf16[4,64,3072]{2,1,0:T(8,128)(2,1)} async-done(((bf16[4,64,768]{2,1,0:T(8,128)(2,1)}), bf16[4,64,3072]{2,1,0:T(8,128)(2,1)}) %all-gather.2.cloned.1.call-update) | async-done | bytes 1572880 | tf_op jit(solution)/shard_map/while/body/eval_jaxpr/all_gather | solution.py:70
  193.5 9.9 %fusion.123 = (f32[4,64]{1,0:T(4,128)}, f32[4,64,2048]{2,1,0:T(8,128)S(1)}) fusion(bf16[1,2,4,64,2048]{4,3,2,1,0:T(8,128)(2,1)S(1)} %copy-done.5, s32[]{:T(128)S(6)} %min.13, bf16[1,2,4,64,2048]{4,3,2,1,0:T(8,128)(2,1)} %get-tuple-element.699, bf16[4,64,3072]{2,1,0:T(8,128)(2,1)} %all-gather.2.cloned.1.call-done, ...), kind=kOutput, calls=%fused_computation.17.clone.1 | convolution fusion | flops 3225943808 | bytes 18351108 | tf_op jit(solution)/shard_map/while/body/eval_jaxpr/scw,fw->scf/dot_general | solution.py:39
  203.3 10.7 %fusion.129 = f32[4,64,3072]{2,1,0:T(8,128)} fusion(bf16[3072,2048]{1,0:T(8,128)(2,1)} %get-tuple-element.701, f32[4,64,2048]{2,1,0:T(8,128)S(1)} %get-tuple-element.640, bf16[1,2,4,64,2048]{4,3,2,1,0:T(8,128)(2,1)S(1)} %copy-done.6, s32[]{:T(128)S(6)} %min.13), kind=kOutput, calls=%fused_computation.2.clone.1 | convolution fusion | flops 3224895488 | bytes 18874372 | tf_op jit(solution)/shard_map/while/body/eval_jaxpr/scf,df->scd/dot_general | solution.py:80
  214.0 11.6 %fusion.130 = f32[4,64,3072]{2,1,0:T(8,128)} fusion(f32[4,64,3072]{2,1,0:T(8,128)} %fusion.129, bf16[3072,2048]{1,0:T(8,128)(2,1)} %get-tuple-element.700, f32[4,64,2048]{2,1,0:T(8,128)} %copy-done.7, bf16[1,2,4,64,2048]{4,3,2,1,0:T(8,128)(2,1)S(1)} %copy-done.6, s32[]{:T(128)S(6)} %min.13, bf16[1,2,4,64,2048]{4,3,2,1,0:T(8,128)(2,1)S(1)} %copy-done.5), kind=kOutput, calls=%fused_computation.8.clone.1 | convolution fusion | flops 3228303360 | bytes 23068676 | tf_op jit(solution)/shard_map/while/body/eval_jaxpr/scf,df->scd/dot_general | solution.py:79
  243.1 20.5 %reduce-scatter.2.cloned.1.call-done = f32[4,64,768]{2,1,0:T(8,128)} async-done(((f32[4,64,3072]{2,1,0:T(8,128)}), f32[4,64,768]{2,1,0:T(8,128)}) %reduce-scatter.2.cloned.1.call-update) | async-done | bytes 786448 | tf_op jit(solution)/shard_map/while/body/eval_jaxpr/reduce_scatter | solution.py:82
  269.8 6.1 %all-reduce.3 = (f32[80,2]{0,1:T(2,128)S(1)}, f32[80,4]{0,1:T(4,128)S(1)}) all-reduce(f32[80,2]{0,1:T(2,128)S(1)} %bitcast.172, f32[80,4]{0,1:T(4,128)S(1)} %fusion.126), channel_id=1, replica_groups=mesh['section'=2,'expert'=4,'tensor'=4] {'tensor'}, use_global_device_ids=true, to_apply=%region_11.11 | all-reduce | flops 480 | bytes 3840 | tf_op jit(solution)/shard_map/while/body/eval_jaxpr/psum | solution.py:97
  276.2 11.9 %all-to-all-done.2 = f32[4,64,768]{2,1,0:T(8,128)S(1)} async-done(((f32[4,64,768]{2,1,0:T(8,128)}), f32[4,64,768]{2,1,0:T(8,128)S(1)}, u32[]{:S(2)}, u32[]{:S(2)}) %all-to-all-start.2) | async-done | bytes 786464 | tf_op jit(solution)/shard_map/while/body/eval_jaxpr/all_to_all | solution.py:84
  306.8 13.6 %all_to_all.47 = bf16[4,64,768]{2,1,0:T(8,128)(2,1)} all-to-all(bf16[4,64,768]{2,1,0:T(8,128)(2,1)S(1)} %bitcast.166), channel_id=1, replica_groups=mesh['section'=2,'expert'=4,'tensor'=4] {'expert'}, dimensions={0} | all-to-all | bytes 786432 | tf_op jit(solution)/shard_map/while/body/eval_jaxpr/all_to_all | solution.py:69
  320.5 17.3 %all-gather.2.cloned.1.call-done = bf16[4,64,3072]{2,1,0:T(8,128)(2,1)} async-done(((bf16[4,64,768]{2,1,0:T(8,128)(2,1)}), bf16[4,64,3072]{2,1,0:T(8,128)(2,1)}) %all-gather.2.cloned.1.call-update) | async-done | bytes 1572880 | tf_op jit(solution)/shard_map/while/body/eval_jaxpr/all_gather | solution.py:70
  337.8 9.9 %fusion.123 = (f32[4,64]{1,0:T(4,128)}, f32[4,64,2048]{2,1,0:T(8,128)S(1)}) fusion(bf16[1,2,4,64,2048]{4,3,2,1,0:T(8,128)(2,1)S(1)} %copy-done.5, s32[]{:T(128)S(6)} %min.13, bf16[1,2,4,64,2048]{4,3,2,1,0:T(8,128)(2,1)} %get-tuple-element.699, bf16[4,64,3072]{2,1,0:T(8,128)(2,1)} %all-gather.2.cloned.1.call-done, ...), kind=kOutput, calls=%fused_computation.17.clone.1 | convolution fusion | flops 3225943808 | bytes 18351108 | tf_op jit(solution)/shard_map/while/body/eval_jaxpr/scw,fw->scf/dot_general | solution.py:39
  347.7 10.7 %fusion.129 = f32[4,64,3072]{2,1,0:T(8,128)} fusion(bf16[3072,2048]{1,0:T(8,128)(2,1)} %get-tuple-element.701, f32[4,64,2048]{2,1,0:T(8,128)S(1)} %get-tuple-element.640, bf16[1,2,4,64,2048]{4,3,2,1,0:T(8,128)(2,1)S(1)} %copy-done.6, s32[]{:T(128)S(6)} %min.13), kind=kOutput, calls=%fused_computation.2.clone.1 | convolution fusion | flops 3224895488 | bytes 18874372 | tf_op jit(solution)/shard_map/while/body/eval_jaxpr/scf,df->scd/dot_general | solution.py:80
  358.4 11.6 %fusion.130 = f32[4,64,3072]{2,1,0:T(8,128)} fusion(f32[4,64,3072]{2,1,0:T(8,128)} %fusion.129, bf16[3072,2048]{1,0:T(8,128)(2,1)} %get-tuple-element.700, f32[4,64,2048]{2,1,0:T(8,128)} %copy-done.7, bf16[1,2,4,64,2048]{4,3,2,1,0:T(8,128)(2,1)S(1)} %copy-done.6, s32[]{:T(128)S(6)} %min.13, bf16[1,2,4,64,2048]{4,3,2,1,0:T(8,128)(2,1)S(1)} %copy-done.5), kind=kOutput, calls=%fused_computation.8.clone.1 | convolution fusion | flops 3228303360 | bytes 23068676 | tf_op jit(solution)/shard_map/while/body/eval_jaxpr/scf,df->scd/dot_general | solution.py:79
  387.5 20.5 %reduce-scatter.2.cloned.1.call-done = f32[4,64,768]{2,1,0:T(8,128)} async-done(((f32[4,64,3072]{2,1,0:T(8,128)}), f32[4,64,768]{2,1,0:T(8,128)}) %reduce-scatter.2.cloned.1.call-update) | async-done | bytes 786448 | tf_op jit(solution)/shard_map/while/body/eval_jaxpr/reduce_scatter | solution.py:82
  420.5 12.0 %all-to-all-done.2 = f32[4,64,768]{2,1,0:T(8,128)S(1)} async-done(((f32[4,64,768]{2,1,0:T(8,128)}), f32[4,64,768]{2,1,0:T(8,128)S(1)}, u32[]{:S(2)}, u32[]{:S(2)}) %all-to-all-start.2) | async-done | bytes 786464 | tf_op jit(solution)/shard_map/while/body/eval_jaxpr/all_to_all | solution.py:84
  (192 shorter events, 135.1 us)
Async XLA Ops:
  7.3 41.9 %copy-start.5 = (bf16[1,2,4,64,2048]{4,3,2,1,0:T(8,128)(2,1)S(1)}, bf16[1,2,4,64,2048]{4,3,2,1,0:T(8,128)(2,1)}, u32[]{:S(2)}) copy-start(bf16[1,2,4,64,2048]{4,3,2,1,0:T(8,128)(2,1)} %get-tuple-element.698) | copy-start | bytes 6291460 | tf_op jit(solution)/shard_map/while
  7.3 41.9 %all-gather.2.cloned.1.call-start = ((), (), s32[]{:S(2)}) async-start(), calls=%async_computation.4 | async-start | bytes 1966080 | tf_op jit(solution)/shard_map/while/body/eval_jaxpr/all_gather | solution.py:70
  30.3 89.0 %reduce-scatter.2.cloned.1.call-start = ((), (), s32[]{:S(2)}) async-start(), calls=%async_computation.5 | async-start | bytes 3932160 | tf_op jit(solution)/shard_map/while/body/eval_jaxpr/reduce_scatter | solution.py:82
  81.4 11.9 %copy-start.4 = (s32[1,2,80,2]{2,3,1,0:T(2,128)S(1)}, s32[1,2,80,2]{2,3,1,0:T(2,128)}, u32[]{:S(2)}) copy-start(s32[1,2,80,2]{2,3,1,0:T(2,128)} %get-tuple-element.694) | copy-start | bytes 3844 | tf_op jit(solution)/shard_map/while
  81.4 69.1 %copy-start.1 = (bf16[2,80,768]{2,1,0:T(8,128)(2,1)S(1)}, bf16[2,80,768]{2,1,0:T(8,128)(2,1)}, u32[]{:S(2)}) copy-start(bf16[2,80,768]{2,1,0:T(8,128)(2,1)} %get-tuple-element.692) | copy-start | bytes 737284 | tf_op jit(solution)/shard_map/while
  88.6 10.3 %all-to-all-start.1 = ((f32[4,1,64]{2,1,0:T(1,128)}), f32[4,1,64]{2,1,0:T(1,128)S(1)}, u32[]{:S(2)}, u32[]{:S(2)}) async-start(f32[4,1,64]{2,1,0:T(1,128)} %bitcast.160), calls=%async_computation.1 | async-start | bytes 4096 | tf_op jit(solution)/shard_map/while/body/eval_jaxpr/all_to_all | solution.py:85
  119.3 24.5 %all-to-all-start.2 = ((f32[4,64,768]{2,1,0:T(8,128)}), f32[4,64,768]{2,1,0:T(8,128)S(1)}, u32[]{:S(2)}, u32[]{:S(2)}) async-start(f32[4,64,768]{2,1,0:T(8,128)} %reduce-scatter.2.cloned.1.call-done), calls=%async_computation.3 | async-start | bytes 1572864 | tf_op jit(solution)/shard_map/while/body/eval_jaxpr/all_to_all | solution.py:84
  150.7 6.8 %collective-permute-start = (bf16[80,768]{1,0:T(8,128)(2,1)S(1)}, bf16[80,768]{1,0:T(8,128)(2,1)S(1)}, u32[]{:S(2)}, u32[]{:S(2)}) collective-permute-start(bf16[80,768]{1,0:T(8,128)(2,1)S(1)} %get-tuple-element.645), channel_id=1, source_target_pairs={{16,0},{17,1},{18,2},{19,3},{20,4},{21,5},{22,6},{23,7},{24,8},{25... | collective-permute-start | bytes 368648 | tf_op jit(solution)/shard_map/while/body/eval_jaxpr/ppermute | solution.py:13
  157.5 36.0 %copy-start.5 = (bf16[1,2,4,64,2048]{4,3,2,1,0:T(8,128)(2,1)S(1)}, bf16[1,2,4,64,2048]{4,3,2,1,0:T(8,128)(2,1)}, u32[]{:S(2)}) copy-start(bf16[1,2,4,64,2048]{4,3,2,1,0:T(8,128)(2,1)} %get-tuple-element.698) | copy-start | bytes 6291460 | tf_op jit(solution)/shard_map/while
  157.5 36.0 %all-gather.2.cloned.1.call-start = ((), (), s32[]{:S(2)}) async-start(), calls=%async_computation.4 | async-start | bytes 1966080 | tf_op jit(solution)/shard_map/while/body/eval_jaxpr/all_gather | solution.py:70
  176.1 87.5 %reduce-scatter.2.cloned.1.call-start = ((), (), s32[]{:S(2)}) async-start(), calls=%async_computation.5 | async-start | bytes 3932160 | tf_op jit(solution)/shard_map/while/body/eval_jaxpr/reduce_scatter | solution.py:82
  225.7 11.9 %copy-start.4 = (s32[1,2,80,2]{2,3,1,0:T(2,128)S(1)}, s32[1,2,80,2]{2,3,1,0:T(2,128)}, u32[]{:S(2)}) copy-start(s32[1,2,80,2]{2,3,1,0:T(2,128)} %get-tuple-element.694) | copy-start | bytes 3844 | tf_op jit(solution)/shard_map/while
  225.7 69.1 %copy-start.1 = (bf16[2,80,768]{2,1,0:T(8,128)(2,1)S(1)}, bf16[2,80,768]{2,1,0:T(8,128)(2,1)}, u32[]{:S(2)}) copy-start(bf16[2,80,768]{2,1,0:T(8,128)(2,1)} %get-tuple-element.692) | copy-start | bytes 737284 | tf_op jit(solution)/shard_map/while
  232.8 10.3 %all-to-all-start.1 = ((f32[4,1,64]{2,1,0:T(1,128)}), f32[4,1,64]{2,1,0:T(1,128)S(1)}, u32[]{:S(2)}, u32[]{:S(2)}) async-start(f32[4,1,64]{2,1,0:T(1,128)} %bitcast.160), calls=%async_computation.1 | async-start | bytes 4096 | tf_op jit(solution)/shard_map/while/body/eval_jaxpr/all_to_all | solution.py:85
  263.6 24.5 %all-to-all-start.2 = ((f32[4,64,768]{2,1,0:T(8,128)}), f32[4,64,768]{2,1,0:T(8,128)S(1)}, u32[]{:S(2)}, u32[]{:S(2)}) async-start(f32[4,64,768]{2,1,0:T(8,128)} %reduce-scatter.2.cloned.1.call-done), calls=%async_computation.3 | async-start | bytes 1572864 | tf_op jit(solution)/shard_map/while/body/eval_jaxpr/all_to_all | solution.py:84
  295.0 6.8 %collective-permute-start = (bf16[80,768]{1,0:T(8,128)(2,1)S(1)}, bf16[80,768]{1,0:T(8,128)(2,1)S(1)}, u32[]{:S(2)}, u32[]{:S(2)}) collective-permute-start(bf16[80,768]{1,0:T(8,128)(2,1)S(1)} %get-tuple-element.645), channel_id=1, source_target_pairs={{16,0},{17,1},{18,2},{19,3},{20,4},{21,5},{22,6},{23,7},{24,8},{25... | collective-permute-start | bytes 368648 | tf_op jit(solution)/shard_map/while/body/eval_jaxpr/ppermute | solution.py:13
  301.8 36.0 %copy-start.5 = (bf16[1,2,4,64,2048]{4,3,2,1,0:T(8,128)(2,1)S(1)}, bf16[1,2,4,64,2048]{4,3,2,1,0:T(8,128)(2,1)}, u32[]{:S(2)}) copy-start(bf16[1,2,4,64,2048]{4,3,2,1,0:T(8,128)(2,1)} %get-tuple-element.698) | copy-start | bytes 6291460 | tf_op jit(solution)/shard_map/while
  301.8 36.0 %all-gather.2.cloned.1.call-start = ((), (), s32[]{:S(2)}) async-start(), calls=%async_computation.4 | async-start | bytes 1966080 | tf_op jit(solution)/shard_map/while/body/eval_jaxpr/all_gather | solution.py:70
  320.4 87.5 %reduce-scatter.2.cloned.1.call-start = ((), (), s32[]{:S(2)}) async-start(), calls=%async_computation.5 | async-start | bytes 3932160 | tf_op jit(solution)/shard_map/while/body/eval_jaxpr/reduce_scatter | solution.py:82
  370.0 11.9 %copy-start.4 = (s32[1,2,80,2]{2,3,1,0:T(2,128)S(1)}, s32[1,2,80,2]{2,3,1,0:T(2,128)}, u32[]{:S(2)}) copy-start(s32[1,2,80,2]{2,3,1,0:T(2,128)} %get-tuple-element.694) | copy-start | bytes 3844 | tf_op jit(solution)/shard_map/while
  370.0 69.1 %copy-start.1 = (bf16[2,80,768]{2,1,0:T(8,128)(2,1)S(1)}, bf16[2,80,768]{2,1,0:T(8,128)(2,1)}, u32[]{:S(2)}) copy-start(bf16[2,80,768]{2,1,0:T(8,128)(2,1)} %get-tuple-element.692) | copy-start | bytes 737284 | tf_op jit(solution)/shard_map/while
  377.2 10.3 %all-to-all-start.1 = ((f32[4,1,64]{2,1,0:T(1,128)}), f32[4,1,64]{2,1,0:T(1,128)S(1)}, u32[]{:S(2)}, u32[]{:S(2)}) async-start(f32[4,1,64]{2,1,0:T(1,128)} %bitcast.160), calls=%async_computation.1 | async-start | bytes 4096 | tf_op jit(solution)/shard_map/while/body/eval_jaxpr/all_to_all | solution.py:85
  407.9 24.5 %all-to-all-start.2 = ((f32[4,64,768]{2,1,0:T(8,128)}), f32[4,64,768]{2,1,0:T(8,128)S(1)}, u32[]{:S(2)}, u32[]{:S(2)}) async-start(f32[4,64,768]{2,1,0:T(8,128)} %reduce-scatter.2.cloned.1.call-done), calls=%async_computation.3 | async-start | bytes 1572864 | tf_op jit(solution)/shard_map/while/body/eval_jaxpr/all_to_all | solution.py:84
  439.3 6.8 %collective-permute-start = (bf16[80,768]{1,0:T(8,128)(2,1)S(1)}, bf16[80,768]{1,0:T(8,128)(2,1)S(1)}, u32[]{:S(2)}, u32[]{:S(2)}) collective-permute-start(bf16[80,768]{1,0:T(8,128)(2,1)S(1)} %get-tuple-element.645), channel_id=1, source_target_pairs={{16,0},{17,1},{18,2},{19,3},{20,4},{21,5},{22,6},{23,7},{24,8},{25... | collective-permute-start | bytes 368648 | tf_op jit(solution)/shard_map/while/body/eval_jaxpr/ppermute | solution.py:13
  (13 other events, 86.1 us)
Sparse Core Ops, SparseCore 0:
  30.4 18.7 all-gather.1
  81.6 37.7 reduce-scatter.1
  176.2 17.1 all-gather.1
  225.8 37.7 reduce-scatter.1
  320.5 17.2 all-gather.1
  370.2 37.7 reduce-scatter.1
where the time goes:
time: 455 us; the launch traced here: 454 us
  waiting for transfers between devices  184 us (40%)
  matrix products  105 us (23%)
  blocking collectives  98.8 us (22%)
  starting transfers between devices  32.2 us (7%)
  between operations  13.4 us (3%)
  other arithmetic  10.5 us (2%)
  local copies, waits for them, and re-layouts  10 us (2%)
    reduce_scatter x3, waiting for transfers between devices, layer_back(): lax.psum_scatter(unit, 'tensor', scatter_dimension=2, tiled=True)  61.5 us
    all_gather x3, waiting for transfers between devices, layer_back(): lax.all_gather(arrived, 'tensor', axis=2, tiled=True)  53.5 us
    all_to_all x3, blocking collectives, layer_back(): lax.all_to_all(copies, 'expert', split_axis=0, concat_axis=0, tiled=True)  45.2 us
    all_to_all x3, waiting for transfers between devices, layer_back(): lax.all_to_all(unit_share, 'expert', split_axis=0, concat_axis=0, tiled=T...  35.9 us
    dot_general x3, matrix products, layer_back(): jnp.einsum('scf,df->scd', gate_grad, gate_mat, preferred_element_type=jnp...  34.9 us
    dot_general x3, matrix products, layer_back(): jnp.einsum('scf,df->scd', up_grad, up_mat, preferred_element_type=jnp.flo...  32.1 us
    dot_general x3, matrix products, add_columns(): jnp.einsum('scw,fw->scf', piece, down_mat, preferred_element_type=jnp.flo...  29.6 us
    psum x3, blocking collectives, layer_back(): prob_grad = lax.psum(prob_part, 'tensor')  18.1 us
  transfers between devices with their start and end apart: 15, of which 15 were waited for; matrix products, arithmetic and copies ran while one was open for 1% of the time, Pallas kernels for 0%

commit v1 on v0

v1 whole, which is shorter than its diff:
```python
import functools

import jax
import jax.numpy as jnp
from jax import lax
from jax.experimental import pallas as pl
from jax.experimental.pallas import tpu as pltpu
from jax.sharding import PartitionSpec as P

norm_eps = 1e-05
MESH = pl.DeviceIdType.MESH
LANES = 128
f32 = jnp.float32
bf16 = jnp.bfloat16


def vmem(count):
    return [pl.BlockSpec(memory_space=pltpu.VMEM)] * count


def remote(src, dst, send_sem, recv_sem, **where):
    return pltpu.make_async_remote_copy(
        src_ref=src,
        dst_ref=dst,
        send_sem=send_sem,
        recv_sem=recv_sem,
        device_id=where,
        device_id_type=MESH,
    )


def greet(places):
    barrier = pltpu.get_barrier_semaphore()
    for place in places:
        pl.semaphore_signal(barrier, inc=1, device_id=place, device_id_type=MESH)
    pl.semaphore_wait(barrier, len(places))


def tensor_place(T):
    t = lax.axis_index("tensor")
    core = lax.rem(t, 2)
    return t, t // 2, core


def exchange_places(H, T):
    z = lax.axis_index("expert")
    t, chip, core = tensor_place(T)
    chips = T // 2
    places = [{"expert": lax.rem(z + k, H)} for k in range(1, H)]
    places += [{"tensor": chip * 2 + 1 - core}]
    places += [{"tensor": lax.rem(chip + j, chips) * 2 + core} for j in range(1, chips)]
    return places


def dispatch_kernel(H, group, T, q, send_ref, out_ref, own_sem, zs, zr, ys, yr, cs, cr):
    z = lax.axis_index("expert")
    t, chip, core = tensor_place(T)
    chips = T // 2
    mate = chip * 2 + 1 - core

    def block(s, tt):
        return out_ref.at[s, :, pl.ds(pl.multiple_of(tt * q, LANES), q)]

    greet(exchange_places(H, T))
    own = pltpu.make_async_copy(send_ref.at[z // group], block(z, t), own_sem)
    own.start()
    far = [own]
    for k in range(1, H):
        h = lax.rem(z + k, H)
        copy = remote(send_ref.at[h // group], block(z, t), zs.at[k], zr.at[k], expert=h)
        copy.start()
        far.append(copy)
    across = {}
    beside = {}

    def relay(k):
        s = lax.rem(z - k + H, H)
        for j in range(1, chips):
            across[k, j].wait_recv()
            here = block(s, lax.rem(chip - j + chips, chips) * 2 + core)
            beside[k, j] = remote(here, here, cs.at[k, j], cr.at[k, j], tensor=mate)
            beside[k, j].start()

    for k in range(H):
        s = lax.rem(z - k + H, H)
        if k == 0:
            own.wait()
        else:
            far[k].wait_recv()
        here = block(s, t)
        for j in range(1, chips):
            to = lax.rem(chip + j, chips) * 2 + core
            across[k, j] = remote(here, here, ys.at[k, j], yr.at[k, j], tensor=to)
            across[k, j].start()
        beside[k, 0] = remote(here, here, cs.at[k, 0], cr.at[k, 0], tensor=mate)
        beside[k, 0].start()
        if k > 0:
            relay(k - 1)
    relay(H - 1)
    for copy in beside.values():
        copy.wait_recv()
    for copy in far[1:] + list(across.values()) + list(beside.values()):
        copy.wait_send()


def dispatch(send, H, T):
    experts, cap, q = send.shape
    group = H // experts
    chips = T // 2
    dma = pltpu.SemaphoreType.DMA
    return pl.pallas_call(
        functools.partial(dispatch_kernel, H, group, T, q),
        out_shape=jax.ShapeDtypeStruct((H, cap, q * T), bf16),
        in_specs=vmem(1),
        out_specs=vmem(1)[0],
        scratch_shapes=[dma, dma((H,)), dma((H,)), dma((H, chips)), dma((H, chips)), dma((H, chips)), dma((H, chips))],
        compiler_params=pltpu.CompilerParams(collective_id=0, has_side_effects=True),
        name="dispatch",
    )(send)


def experts_kernel(steps, micro_ref, rows_ref, down_ref, gate_ref, up_ref, ga_ref, ua_ref, out_ref, w_ref, acc):
    step = pl.program_id(0)
    nt = (((1,), (1,)), ((), ()))
    count = rows_ref.shape[0]
    wide = down_ref.shape[0]
    v = lax.dot_general(rows_ref[...], down_ref[...], nt, preferred_element_type=f32)
    a = ga_ref[...].reshape(count, wide).astype(f32)
    b = ua_ref[...].reshape(count, wide).astype(f32)
    sg = jax.nn.sigmoid(a)
    swish = a * sg
    vb = v * b
    part = jnp.sum(swish * vb, axis=-1, keepdims=True)
    da = (vb * (sg * (1.0 + a * (1.0 - sg)))).astype(bf16)
    db = (v * swish).astype(bf16)

    @pl.when(step == 0)
    def _():
        w_ref[...] = jnp.broadcast_to(part, w_ref.shape)

    @pl.when(step > 0)
    def _():
        w_ref[...] += jnp.broadcast_to(part, w_ref.shape)

    width = out_ref.shape[1]
    tile = 256 * max(1, width // 256 // 4) if width % 256 == 0 else width
    while width % tile:
        tile -= 256
    for low in range(0, width, tile):
        at = slice(low, low + tile)
        u = lax.dot_general(da, gate_ref[at, :], nt, preferred_element_type=f32)
        u = u + lax.dot_general(db, up_ref[at, :], nt, preferred_element_type=f32)

        @pl.when(step == 0)
        def _():
            acc[:, at] = u

        @pl.when(step > 0)
        def _():
            acc[:, at] += u

    @pl.when(step == steps - 1)
    def _():
        out_ref[...] = acc[...].astype(bf16)


def expert_backward(micro, rows, down, gate, up, saved_gate, saved_up):
    count, width = rows.shape
    units = down.shape[0]
    _, H, cap, _ = saved_gate.shape
    wide = min(256, units)
    steps = units // wide
    whole = lambda j, m: (0, 0)
    act = pl.BlockSpec((1, H, cap, wide), lambda j, m: (m[0], 0, 0, j))
    return pl.pallas_call(
        functools.partial(experts_kernel, steps),
        out_shape=(
            jax.ShapeDtypeStruct((count, width), bf16),
            jax.ShapeDtypeStruct((count, LANES), f32),
        ),
        grid_spec=pltpu.PrefetchScalarGridSpec(
            num_scalar_prefetch=1,
            grid=(steps,),
            in_specs=[
                pl.BlockSpec((count, width), whole),
                pl.BlockSpec((wide, width), lambda j, m: (j, 0)),
                pl.BlockSpec((width, wide), lambda j, m: (0, j)),
                pl.BlockSpec((width, wide), lambda j, m: (0, j)),
                act,
                act,
            ],
            out_specs=[pl.BlockSpec((count, width), whole), pl.BlockSpec((count, LANES), whole)],
            scratch_shapes=[pltpu.VMEM((count, width), f32)],
        ),
        compiler_params=pltpu.CompilerParams(vmem_limit_bytes=60 * 1024 * 1024),
        name="experts",
    )(micro, rows, down, gate, up, saved_gate, saved_up)


def combine_kernel(
    H, T, q, part_ref, w_ref, out_ref, wout_ref, rx1, tx2, rx2, tx3,
    own_sem, ws, wr, cs, cr, ys, yr, zs, zr,
):
    z = lax.axis_index("expert")
    t, chip, core = tensor_place(T)
    chips = T // 2
    mate = chip * 2 + 1 - core
    order = list(range(1, H)) + [0]

    def cols(tt):
        return pl.ds(pl.multiple_of(tt * q, LANES), q)

    greet(exchange_places(H, T))
    own = pltpu.make_async_copy(w_ref.at[z], wout_ref.at[z], own_sem)
    own.start()
    first = {}
    for k in order:
        s = lax.rem(z + k, H)
        for j in list(range(1, chips)) + [0]:
            theirs = lax.rem(chip + j, chips) * 2 + 1 - core
            first[k, j] = remote(
                part_ref.at[s, :, cols(theirs)], rx1.at[k, j], cs.at[k, j], cr.at[k, j], tensor=mate
            )
            first[k, j].start()
    weights = []
    for k in range(1, H):
        h = lax.rem(z + k, H)
        copy = remote(w_ref.at[h], wout_ref.at[z], ws.at[k], wr.at[k], expert=h)
        copy.start()
        weights.append(copy)
    second = {}
    for k in order:
        s = lax.rem(z + k, H)
        for j in range(1, chips):
            to = lax.rem(chip + j, chips) * 2 + core
            first[k, j].wait_recv()
            tx2[k, j] = (part_ref[s, :, cols(to)].astype(f32) + rx1[k, j].astype(f32)).astype(bf16)
            second[k, j] = remote(tx2.at[k, j], rx2.at[k, j], ys.at[k, j], yr.at[k, j], tensor=to)
            second[k, j].start()
    third = []
    for k in order:
        s = lax.rem(z + k, H)
        first[k, 0].wait_recv()
        total = part_ref[s, :, cols(t)].astype(f32) + rx1[k, 0].astype(f32)
        for j in range(1, chips):
            second[k, j].wait_recv()
            total = total + rx2[k, j].astype(f32)
        if k == 0:
            out_ref[z] = total.astype(bf16)
        else:
            tx3[k] = total.astype(bf16)
            copy = remote(tx3.at[k], out_ref.at[z], zs.at[k], zr.at[k], expert=s)
            copy.start()
            third.append(copy)
    own.wait()
    for copy in weights + third:
        copy.wait_recv()
    for copy in list(first.values()) + list(second.values()) + weights + third:
        copy.wait_send()


def combine(part, weights, T):
    H, cap, width = part.shape
    q = width // T
    chips = T // 2
    dma = pltpu.SemaphoreType.DMA
    many = lambda: dma((H, chips))
    return pl.pallas_call(
        functools.partial(combine_kernel, H, T, q),
        out_shape=(
            jax.ShapeDtypeStruct((H, cap, q), bf16),
            jax.ShapeDtypeStruct(weights.shape, f32),
        ),
        in_specs=vmem(2),
        out_specs=tuple(vmem(2)),
        scratch_shapes=[
            pltpu.VMEM((H, chips, cap, q), bf16),
            pltpu.VMEM((H, chips, cap, q), bf16),
            pltpu.VMEM((H, chips, cap, q), bf16),
            pltpu.VMEM((H, cap, q), bf16),
            dma, dma((H,)), dma((H,)), many(), many(), many(), many(), dma((H,)), dma((H,)),
        ],
        compiler_params=pltpu.CompilerParams(collective_id=1, has_side_effects=True),
        name="combine",
    )(part, weights)


def share(T, tx, rx, ss, rs):
    t = lax.axis_index("tensor")
    copies = []
    for k in range(1, T):
        copy = remote(tx, rx.at[k], ss.at[k], rs.at[k], tensor=lax.rem(t + k, T))
        copy.start()
        copies.append(copy)
    return copies


def tensor_sum_kernel(T, x_ref, out_ref, rx, ss, rs):
    t = lax.axis_index("tensor")
    greet([{"tensor": lax.rem(t + k, T)} for k in range(1, T)])
    copies = share(T, x_ref, rx, ss, rs)
    total = x_ref[...]
    for k, copy in enumerate(copies, 1):
        copy.wait_recv()
        total = total + rx[k]
    out_ref[...] = total
    for copy in copies:
        copy.wait_send()


def tensor_sum(x, T, number):
    rows, lanes = x.shape
    high, long = -(-rows // 8) * 8, -(-lanes // LANES) * LANES
    padded = jnp.pad(x, ((0, high - rows), (0, long - lanes)))
    dma = pltpu.SemaphoreType.DMA
    total = pl.pallas_call(
        functools.partial(tensor_sum_kernel, T),
        out_shape=jax.ShapeDtypeStruct(padded.shape, f32),
        in_specs=vmem(1),
        out_specs=vmem(1)[0],
        scratch_shapes=[pltpu.VMEM((T,) + padded.shape, f32), dma((T,)), dma((T,))],
        compiler_params=pltpu.CompilerParams(collective_id=number, has_side_effects=True),
        name="tensor_sum",
    )(padded)
    return total[:rows, :lanes]


def finish_kernel(
    T, S, width_all, hot_ref, units_ref, prob_ref, aux_ref, step_ref, x_ref, up_ref, gain_ref,
    out_ref, in_ref, tx, rx, ss, rs, send_sem, recv_sem,
):
    t = lax.axis_index("tensor")
    p = lax.axis_index("section")
    below = lax.rem(p + S - 1, S)
    above = lax.rem(p + 1, S)
    places = [{"tensor": lax.rem(t + k, T)} for k in range(1, T)]
    if S > 1:
        places.append({"section": above})
    greet(places)
    tokens = x_ref.shape[0]
    both = jnp.dot(hot_ref[...], units_ref[...], preferred_element_type=f32)
    aux = aux_ref[...]
    q0, q1 = aux[:, 0:1], aux[:, 1:2]
    scale, cross = aux[:, 2:3], aux[:, 3:4]
    values = x_ref[...].astype(f32)
    gain = gain_ref[...]
    hidden = q0 * both[:tokens] + q1 * both[tokens:]
    gained = hidden * gain
    moment = jnp.sum(values * gained, axis=-1, keepdims=True)
    lane = lax.broadcasted_iota(jnp.int32, prob_ref.shape, 1)
    tx[...] = jnp.where(lane == 1, moment, prob_ref[...])
    copies = share(T, tx, rx, ss, rs)
    total = tx[...]
    for k, copy in enumerate(copies, 1):
        copy.wait_recv()
        total = total + rx[k]
    step = q0 * q1 * total[:, 0:1]
    mean = (total[:, 1:2] + step * cross) / width_all
    result = (
        up_ref[...].astype(f32)
        + scale * (gained + (step * step_ref[...]) * gain)
        - values * (scale * scale * scale * mean)
    )
    out_ref[...] = result.astype(bf16)
    if S > 1:
        onward = remote(out_ref, in_ref, send_sem, recv_sem, section=below)
        onward.start()
        onward.wait()
    else:
        in_ref[...] = out_ref[...]
    for copy in copies:
        copy.wait_send()


def finish(T, S, hot, units, prob, aux, step, x, up, gain):
    tokens, q = x.shape
    shape = jax.ShapeDtypeStruct((tokens, q), bf16)
    dma = pltpu.SemaphoreType.DMA
    return pl.pallas_call(
        functools.partial(finish_kernel, T, S, q * T),
        out_shape=(shape, shape),
        in_specs=vmem(8),
        out_specs=tuple(vmem(2)),
        scratch_shapes=[
            pltpu.VMEM((tokens, LANES), f32),
            pltpu.VMEM((T, tokens, LANES), f32),
            dma((T,)), dma((T,)), dma, dma,
        ],
        compiler_params=pltpu.CompilerParams(collective_id=2, has_side_effects=True),
        name="finish",
    )(hot, units, prob, aux, step, x, up, gain)


def on_device(
    layer_inputs, grad_out, norm_gain, router_w, w_gate, w_up, w_down, saved_gate, saved_up, routes
):
    S = lax.axis_size("section")
    H = lax.axis_size("expert")
    T = lax.axis_size("tensor")
    position = lax.axis_index("section")
    micros, tokens, q = grad_out.shape
    gain = norm_gain[0].astype(f32)
    router = router_w[0]
    width = w_gate.shape[1]
    experts = router.shape[1]
    group = H // experts
    cap = saved_gate.shape[3]
    slots = experts * cap
    highest = lax.Precision.HIGHEST

    values = layer_inputs[0].astype(f32)
    router32 = router.astype(f32)
    gained_router = gain[:, None] * router32
    squares = jnp.sum(values * values, axis=-1).reshape(1, micros * tokens)
    crossing = jnp.einsum("mtd,de->emt", values, gained_router, precision=highest)
    stats = jnp.concatenate([squares, crossing.reshape(experts, micros * tokens)], axis=0)
    stats = tensor_sum(stats, T, 3)
    scale = lax.rsqrt(stats[0].reshape(micros, tokens) / width + norm_eps)
    crossing = stats[1:].reshape(experts, micros, tokens).transpose(1, 2, 0)
    normed = (values * scale[:, :, None] * gain).astype(bf16)
    logits = jnp.einsum("mtd,de->emt", normed, router, preferred_element_type=f32)
    logits = tensor_sum(logits.reshape(experts, micros * tokens), T, 4)
    logits = logits.reshape(experts, micros, tokens).transpose(1, 2, 0)

    chosen = routes[0]
    expert_ids = jnp.arange(experts, dtype=jnp.int32)
    onehot = (chosen[..., None] == expert_ids).astype(f32)
    picked = jnp.sum(onehot * logits[:, :, None, :], axis=-1)
    first = jax.nn.sigmoid(picked[..., 0] - picked[..., 1])
    second = jax.nn.sigmoid(picked[..., 1] - picked[..., 0])
    lean = onehot[:, :, 0] - onehot[:, :, 1]
    cross = jnp.sum(lean * crossing, axis=-1)
    steps = jnp.einsum("mte,de->mtd", lean, router32, precision=highest)
    flat = onehot.reshape(micros, tokens * 2, experts)
    earlier = jnp.cumsum(flat, axis=1) - flat
    within = jnp.sum(earlier * flat, axis=-1).astype(jnp.int32).reshape(micros, tokens, 2)
    target = (chosen * cap + within).transpose(0, 2, 1)
    slot_ids = jnp.arange(slots, dtype=jnp.int32)
    hot = target[..., None] == slot_ids
    select = jnp.any(hot, axis=1).astype(bf16)
    hot = hot.astype(bf16)
    wide_hot = jnp.broadcast_to(
        hot.reshape(micros, 2, tokens, experts, 1, cap), (micros, 2, tokens, experts, group, cap)
    ).reshape(micros, 2 * tokens, H * cap)
    hot_lean = (hot[:, 0].astype(f32) - hot[:, 1].astype(f32))
    aux = jnp.stack([first, second, scale, cross], axis=-1)
    aux = jnp.pad(aux, ((0, 0), (0, 0), (0, LANES - 4)))

    def pick(array, number):
        return lax.dynamic_index_in_dim(array, number, 0, keepdims=False)

    lanes = -(-cap // LANES) * LANES
    incoming = jnp.zeros((tokens, q), bf16)
    grads = jnp.zeros((micros, tokens, q), bf16)
    for tick in range(micros + S - 1):
        number = tick - (S - 1 - position)
        valid = jnp.logical_and(number >= 0, number < micros)
        safe = jnp.clip(number, 0, micros - 1)
        upstream = jnp.where(position == S - 1, pick(grad_out, safe), incoming)
        send = lax.dot_general(
            pick(select, safe), upstream, (((0,), (0,)), ((), ())), preferred_element_type=f32
        ).astype(bf16)
        rows = dispatch(send.reshape(experts, cap, q), H, T).reshape(H * cap, width)
        part, weight = expert_backward(
            safe[None].astype(jnp.int32), rows, w_down[0], w_gate[0], w_up[0], saved_gate[0], saved_up[0]
        )
        weight = weight[:, 0].reshape(H, 1, cap)
        weight = jnp.pad(weight, ((0, 0), (0, 7), (0, lanes - cap)))
        units, weight = combine(part.reshape(H, cap, width), weight, T)
        weight = jnp.sum(weight[:, 0, :cap].reshape(experts, group, cap), axis=1).reshape(slots)
        prob = jnp.sum(pick(hot_lean, safe) * weight[None, :], axis=-1, keepdims=True)
        prob = jnp.pad(prob, ((0, 0), (0, LANES - 1)))
        result, incoming = finish(
            T, S, pick(wide_hot, safe), units.reshape(H * cap, q), prob, pick(aux, safe),
            pick(steps, safe), pick(layer_inputs[0], safe), upstream, gain[None, :],
        )
        updated = lax.dynamic_update_index_in_dim(grads, result, safe, 0)
        grads = jnp.where(valid, updated, grads)
    return grads[None]


def solution(mesh):
    placed = (
        P("section", None, "expert", "tensor"),
        P(None, "expert", "tensor"),
        P("section", "tensor"),
        P("section", "tensor", None),
        P("section", None, ("expert", "tensor")),
        P("section", None, ("expert", "tensor")),
        P("section", ("expert", "tensor"), None),
        P("section", None, None, None, ("expert", "tensor")),
        P("section", None, None, None, ("expert", "tensor")),
        P("section", None, "expert", None),
    )
    return jax.shard_map(
        on_device,
        mesh=mesh,
        in_specs=placed,
        out_specs=P("section", None, "expert", "tensor"),
        check_vma=False,
    )
```

time: 455 us -> 304 us (0.67)
  Pallas kernels: 0 us -> 268 us
  waiting for transfers between devices: 184 us -> 0 us
  matrix products: 105 us -> 4.04 us
  blocking collectives: 98.8 us -> 0 us
  starting transfers between devices: 32.2 us -> 0 us
  between operations: 13.4 us -> 0.41 us
  local copies, waits for them, and re-layouts: 10 us -> 20 us
    pallas_call x0 -> x14, Pallas kernels: none -> 268 us  [the longest x3 99 us: expert_backward(): pl.pallas_call(functools.partial(experts_kernel, steps), out_shape=(jax.S...]
    dot_general x24 -> x6, matrix products: 105 us -> 4.04 us  [the longest x3 3.16 us: on_device(): lax.dot_general(pick(select, safe), upstream, (((0,), (0,)), ((), ())), p...]
    reduce_scatter x3 -> x0, waiting for transfers between devices: 61.5 us -> none  [layer_back(): lax.psum_scatter(unit, 'tensor', scatter_dimension=2, tiled=True)]
    psum x9 -> x0, blocking collectives: 53.6 us -> none  [the longest x3 18.1 us: layer_back(): prob_grad = lax.psum(prob_part, 'tensor')]
    all_gather x3 -> x0, waiting for transfers between devices: 53.5 us -> none  [layer_back(): lax.all_gather(arrived, 'tensor', axis=2, tiled=True)]
    all_to_all x6 -> x0, waiting for transfers between devices: 52.3 us -> none  [the longest x3 35.9 us: layer_back(): lax.all_to_all(unit_share, 'expert', split_axis=0, concat_axis=0, tiled=T...]
    all_to_all x3 -> x0, blocking collectives: 45.2 us -> none  [layer_back(): lax.all_to_all(copies, 'expert', split_axis=0, concat_axis=0, tiled=True)]
    all_to_all x6 -> x0, starting transfers between devices: 28.1 us -> none  [the longest x3 14.4 us: layer_back(): lax.all_to_all(weight_part, 'expert', split_axis=0, concat_axis=0, tiled=...]
  transfers between devices with their start and end apart: 15 -> 0, of which waited for: 15 -> 0; matrix products, arithmetic and copies ran while one was open for 1% -> 0% of each run, Pallas kernels for 0% -> 0%
where the time goes in v1:
time: 304 us; the launch traced here: 303 us
  Pallas kernels  268 us (88%)
  local copies, waits for them, and re-layouts  20 us (7%)
  other arithmetic  10.5 us (3%)
  matrix products  4.04 us (1%)
    pallas_call x3, Pallas kernels, expert_backward(): pl.pallas_call(functools.partial(experts_kernel, steps), out_shape=(jax.S...  99 us
    pallas_call x3, Pallas kernels, combine(): pl.pallas_call(functools.partial(combine_kernel, H, T, q), out_shape=(jax...  63 us
    pallas_call x3, Pallas kernels, dispatch(): pl.pallas_call(functools.partial(dispatch_kernel, H, group, T, q), out_sh...  60.9 us
    pallas_call x3, Pallas kernels, finish(): pl.pallas_call(functools.partial(finish_kernel, T, S, q * T), out_shape=(...  35.5 us
    pallas_call x2, Pallas kernels, tensor_sum(): pl.pallas_call(functools.partial(tensor_sum_kernel, T), out_shape=jax.Sha...  10 us

profile of v1, /device:TPU:0, one launch (start us, length us, event | category | flops | bytes accessed | tf_op | source)
XLA Modules:
  0.0 303.3 jit_solution(14652816940150131289)
XLA Ops:
  1.9 2.4 reduce-window.6
  5.2 1.1 convolution_convert_fusion.2
  6.3 22.1 %dispatch.3 = bf16[4,64,3072]{2,1,0:T(8,128)(2,1)} custom-call(bf16[4,64,768]{2,1,0:T(8,128)(2,1)} %bitcast.150), custom_call_target="tpu_custom_call" | custom-call | tf_op jit(solution)/shard_map/dispatch/pallas_call | solution.py:111
  28.3 32.9 %experts.3 = (bf16[256,3072]{1,0:T(8,128)(2,1)}, f32[256,128]{1,0:T(8,128)}) custom-call(s32[1]{0:T(128)} %bitcast.5.micro_ref, bf16[256,3072]{1,0:T(8,128)(2,1)} %bitcast.141, bf16[2048,3072]{1,0:T(8,128)(2,1)} %bitcast.126, bf16[3072,2048]{1,0:T(8,128)(2,1)} %bitcast.129, bf16[3072,2048]{1,0:T(8,128)(2,1)} %bitcast.132, ...), custom_call_target="tpu_custom_call" | custom-call | tf_op jit(solution)/shard_map/experts/pallas_call | solution.py:175
  61.3 1.1 slice_reduce_fusion.2
  63.0 21.5 %combine.3 = (bf16[4,64,768]{2,1,0:T(8,128)(2,1)}, f32[4,8,128]{2,1,0:T(8,128)}) custom-call(bf16[4,64,3072]{2,1,0:T(8,128)(2,1)} %bitcast.146, f32[4,8,128]{2,1,0:T(8,128)} %pad.37.w_ref), custom_call_target="tpu_custom_call" | custom-call | tf_op jit(solution)/shard_map/combine/pallas_call | solution.py:268
  87.5 5.0 %tensor_sum.2 = f32[8,256]{1,0:T(8,128)} custom-call(f32[8,256]{1,0:T(8,128)} %select_maximum_fusion.3.x_ref), custom_call_target="tpu_custom_call" | custom-call | tf_op jit(solution)/shard_map/tensor_sum/pallas_call | solution.py:316
  93.0 1.4 fusion.37
  95.5 5.0 %tensor_sum.3 = f32[8,256]{1,0:T(8,128)} custom-call(f32[8,256]{1,0:T(8,128)} %pad.40.x_ref), custom_call_target="tpu_custom_call" | custom-call | tf_op jit(solution)/shard_map/tensor_sum/pallas_call | solution.py:316
  106.9 12.2 %finish.3 = (bf16[80,768]{1,0:T(8,128)(2,1)}, bf16[80,768]{1,0:T(8,128)(2,1)}) custom-call(bf16[160,256]{1,0:T(8,128)(2,1)} %get-tuple-element.49.hot_ref, bf16[256,768]{1,0:T(8,128)(2,1)} %bitcast.153, f32[80,128]{1,0:T(8,128)} %pad.38.prob_ref, f32[80,128]{1,0:T(8,128)} %bitcast.156, f32[80,768]{1,0:T(8,128)} %get-tuple-element.43.step_ref, ...), custom_call_target="tpu_custom_call" | custom-call | tf_op jit(solution)/shard_map/finish/pallas_call | solution.py:379
  119.0 0.9 bitcast_select_fusion.3.up_ref
  120.0 1.1 convolution_convert_fusion.1
  121.0 19.4 %dispatch.4 = bf16[4,64,3072]{2,1,0:T(8,128)(2,1)} custom-call(bf16[4,64,768]{2,1,0:T(8,128)(2,1)} %bitcast.151), custom_call_target="tpu_custom_call" | custom-call | tf_op jit(solution)/shard_map/dispatch/pallas_call | solution.py:111
  140.4 32.9 %experts.4 = (bf16[256,3072]{1,0:T(8,128)(2,1)}, f32[256,128]{1,0:T(8,128)}) custom-call(s32[1]{0:T(128)} %bitcast.35.micro_ref, bf16[256,3072]{1,0:T(8,128)(2,1)} %bitcast.142, bf16[2048,3072]{1,0:T(8,128)(2,1)} %bitcast.127, bf16[3072,2048]{1,0:T(8,128)(2,1)} %bitcast.130, bf16[3072,2048]{1,0:T(8,128)(2,1)} %bitcast.133, ...), custom_call_target="tpu_custom_call" | custom-call | tf_op jit(solution)/shard_map/experts/pallas_call | solution.py:175
  173.4 1.0 slice_reduce_fusion.1
  175.1 20.7 %combine.4 = (bf16[4,64,768]{2,1,0:T(8,128)(2,1)}, f32[4,8,128]{2,1,0:T(8,128)}) custom-call(bf16[4,64,3072]{2,1,0:T(8,128)(2,1)} %bitcast.147, f32[4,8,128]{2,1,0:T(8,128)} %pad.42.w_ref), custom_call_target="tpu_custom_call" | custom-call | tf_op jit(solution)/shard_map/combine/pallas_call | solution.py:268
  198.2 11.7 %finish.4 = (bf16[80,768]{1,0:T(8,128)(2,1)}, bf16[80,768]{1,0:T(8,128)(2,1)}) custom-call(bf16[160,256]{1,0:T(8,128)(2,1)} %get-tuple-element.48.hot_ref, bf16[256,768]{1,0:T(8,128)(2,1)} %bitcast.155, f32[80,128]{1,0:T(8,128)} %pad.43.prob_ref, f32[80,128]{1,0:T(8,128)} %bitcast.158, f32[80,768]{1,0:T(8,128)} %get-tuple-element.42.step_ref, ...), custom_call_target="tpu_custom_call" | custom-call | tf_op jit(solution)/shard_map/finish/pallas_call | solution.py:379
  210.8 1.1 convolution_convert_fusion
  211.9 19.4 %dispatch.5 = bf16[4,64,3072]{2,1,0:T(8,128)(2,1)} custom-call(bf16[4,64,768]{2,1,0:T(8,128)(2,1)} %bitcast.149), custom_call_target="tpu_custom_call" | custom-call | tf_op jit(solution)/shard_map/dispatch/pallas_call | solution.py:111
  231.3 33.1 %experts.5 = (bf16[256,3072]{1,0:T(8,128)(2,1)}, f32[256,128]{1,0:T(8,128)}) custom-call(s32[1]{0:T(128)} %bitcast.51.micro_ref, bf16[256,3072]{1,0:T(8,128)(2,1)} %bitcast.143, bf16[2048,3072]{1,0:T(8,128)(2,1)} %bitcast.128, bf16[3072,2048]{1,0:T(8,128)(2,1)} %bitcast.131, bf16[3072,2048]{1,0:T(8,128)(2,1)} %bitcast.134, ...), custom_call_target="tpu_custom_call" | custom-call | tf_op jit(solution)/shard_map/experts/pallas_call | solution.py:175
  264.4 1.0 slice_reduce_fusion
  266.1 20.7 %combine.5 = (bf16[4,64,768]{2,1,0:T(8,128)(2,1)}, f32[4,8,128]{2,1,0:T(8,128)}) custom-call(bf16[4,64,3072]{2,1,0:T(8,128)(2,1)} %bitcast.148, f32[4,8,128]{2,1,0:T(8,128)} %pad.44.w_ref), custom_call_target="tpu_custom_call" | custom-call | tf_op jit(solution)/shard_map/combine/pallas_call | solution.py:268
  289.2 11.6 %finish.5 = (bf16[80,768]{1,0:T(8,128)(2,1)}, bf16[80,768]{1,0:T(8,128)(2,1)}) custom-call(bf16[160,256]{1,0:T(8,128)(2,1)} %get-tuple-element.47.hot_ref, bf16[256,768]{1,0:T(8,128)(2,1)} %bitcast.154, f32[80,128]{1,0:T(8,128)} %pad.45.prob_ref, f32[80,128]{1,0:T(8,128)} %bitcast.157, f32[80,768]{1,0:T(8,128)} %get-tuple-element.41.step_ref, ...), custom_call_target="tpu_custom_call" | custom-call | tf_op jit(solution)/shard_map/finish/pallas_call | solution.py:379
  301.7 1.6 bitcast_dynamic-update-slice_fusion
  (98 shorter events, 22.1 us)
Async XLA Ops:
  0.9 27.4 %copy-start.1 = (bf16[80,768]{1,0:T(8,128)(2,1)}, bf16[80,768]{1,0:T(8,128)(2,1)S(1)}, u32[]{:S(2)}) copy-start(bf16[80,768]{1,0:T(8,128)(2,1)S(1)} %select_bitcast_fusion.up_ref) | copy-start | bytes 368644
  61.3 25.0 %copy-start.8 = (bf16[1,768]{1,0:T(2,128)(2,1)S(1)}, bf16[1,768]{1,0:T(2,128)(2,1)}, u32[]{:S(2)}) copy-start(bf16[1,768]{1,0:T(2,128)(2,1)} %param.12) | copy-start | bytes 4612
  61.3 25.0 %copy-start = (bf16[1,2,80,768]{3,2,1,0:T(8,128)(2,1)S(1)}, bf16[1,2,80,768]{3,2,1,0:T(8,128)(2,1)}, u32[]{:S(2)}) copy-start(bf16[1,2,80,768]{3,2,1,0:T(8,128)(2,1)} %param.10) | copy-start | bytes 737284
  61.3 25.0 %copy-start.7 = (bf16[1,768,4]{1,2,0:T(4,128)(2,1)S(1)}, bf16[1,768,4]{1,2,0:T(4,128)(2,1)}, u32[]{:S(2)}) copy-start(bf16[1,768,4]{1,2,0:T(4,128)(2,1)} %param.13) | copy-start | bytes 18436
  104.6 14.5 %copy-start.4 = (bf16[2,80,768]{2,1,0:T(8,128)(2,1)S(1)}, bf16[2,80,768]{2,1,0:T(8,128)(2,1)}, u32[]{:S(2)}) copy-start(bf16[2,80,768]{2,1,0:T(8,128)(2,1)} %param.11) | copy-start | bytes 737284
  120.0 53.4 %copy-start.3 = (bf16[80,768]{1,0:T(8,128)(2,1)}, bf16[80,768]{1,0:T(8,128)(2,1)S(1)}, u32[]{:S(2)}) copy-start(bf16[80,768]{1,0:T(8,128)(2,1)S(1)} %bitcast_select_fusion.3.up_ref) | copy-start | bytes 368644
  210.8 53.6 %copy-start.2 = (bf16[80,768]{1,0:T(8,128)(2,1)}, bf16[80,768]{1,0:T(8,128)(2,1)S(1)}, u32[]{:S(2)}) copy-start(bf16[80,768]{1,0:T(8,128)(2,1)S(1)} %bitcast_select_fusion.1.up_ref) | copy-start | bytes 368644
  266.1 34.8 %copy-start.5 = (bf16[80,768]{1,0:T(8,128)(2,1)S(1)}, bf16[80,768]{1,0:T(8,128)(2,1)}, u32[]{:S(2)}) copy-start(bf16[80,768]{1,0:T(8,128)(2,1)} %get-tuple-element.26) | copy-start | bytes 368644
  266.1 34.9 %copy-start.6 = (bf16[80,768]{1,0:T(8,128)(2,1)S(1)}, bf16[80,768]{1,0:T(8,128)(2,1)}, u32[]{:S(2)}) copy-start(bf16[80,768]{1,0:T(8,128)(2,1)} %get-tuple-element.32) | copy-start | bytes 368644

commit v2 on v1

--- a/solution.py
+++ b/solution.py
@@ -122,7 +122,7 @@
 def experts_kernel(steps, micro_ref, rows_ref, down_ref, gate_ref, up_ref, ga_ref, ua_ref, out_ref, w_ref, acc):
     step = pl.program_id(0)
     nt = (((1,), (1,)), ((), ()))
-    count = rows_ref.shape[0]
+    count, width = rows_ref.shape
     wide = down_ref.shape[0]
     v = lax.dot_general(rows_ref[...], down_ref[...], nt, preferred_element_type=f32)
     a = ga_ref[...].reshape(count, wide).astype(f32)
@@ -133,42 +133,34 @@
     part = jnp.sum(swish * vb, axis=-1, keepdims=True)
     da = (vb * (sg * (1.0 + a * (1.0 - sg)))).astype(bf16)
     db = (v * swish).astype(bf16)
+    dab = jnp.concatenate([da, db], axis=1)
 
     @pl.when(step == 0)
     def _():
         w_ref[...] = jnp.broadcast_to(part, w_ref.shape)
+        acc[...] = jnp.zeros_like(acc)
 
     @pl.when(step > 0)
     def _():
         w_ref[...] += jnp.broadcast_to(part, w_ref.shape)
 
-    width = out_ref.shape[1]
-    tile = 256 * max(1, width // 256 // 4) if width % 256 == 0 else width
-    while width % tile:
-        tile -= 256
+    tile = next(n for n in (256, 768, 512, 384, 256, 128, width) if width % n == 0)
     for low in range(0, width, tile):
         at = slice(low, low + tile)
-        u = lax.dot_general(da, gate_ref[at, :], nt, preferred_element_type=f32)
-        u = u + lax.dot_general(db, up_ref[at, :], nt, preferred_element_type=f32)
-
-        @pl.when(step == 0)
-        def _():
-            acc[:, at] = u
-
-        @pl.when(step > 0)
-        def _():
-            acc[:, at] += u
+        acc[:, at] += lax.dot_general(dab, jnp.concatenate([gate_ref[at, :], up_ref[at, :]], axis=1), nt, preferred_element_type=f32)
 
     @pl.when(step == steps - 1)
     def _():
-        out_ref[...] = acc[...].astype(bf16)
+        for low in range(0, width, LANES):
+            at = slice(low, low + LANES)
+            out_ref[:, at] = acc[:, at].astype(bf16)
 
 
 def expert_backward(micro, rows, down, gate, up, saved_gate, saved_up):
     count, width = rows.shape
     units = down.shape[0]
     _, H, cap, _ = saved_gate.shape
-    wide = min(256, units)
+    wide = min(512 if count <= 512 else 256, units)
     steps = units // wide
     whole = lambda j, m: (0, 0)
     act = pl.BlockSpec((1, H, cap, wide), lambda j, m: (m[0], 0, 0, j))
@@ -326,7 +318,7 @@
 
 
 def finish_kernel(
-    T, S, width_all, hot_ref, units_ref, prob_ref, aux_ref, step_ref, x_ref, up_ref, gain_ref,
+    T, S, width_all, onward_too, hot_ref, units_ref, prob_ref, aux_ref, step_ref, x_ref, up_ref, gain_ref,
     out_ref, in_ref, tx, rx, ss, rs, send_sem, recv_sem,
 ):
     t = lax.axis_index("tensor")
@@ -334,7 +326,7 @@
     below = lax.rem(p + S - 1, S)
     above = lax.rem(p + 1, S)
     places = [{"tensor": lax.rem(t + k, T)} for k in range(1, T)]
-    if S > 1:
+    if onward_too:
         places.append({"section": above})
     greet(places)
     tokens = x_ref.shape[0]
@@ -362,22 +354,22 @@
         - values * (scale * scale * scale * mean)
     )
     out_ref[...] = result.astype(bf16)
-    if S > 1:
+    if onward_too:
         onward = remote(out_ref, in_ref, send_sem, recv_sem, section=below)
         onward.start()
         onward.wait()
     else:
-        in_ref[...] = out_ref[...]
+        in_ref[...] = jnp.zeros_like(in_ref)
     for copy in copies:
         copy.wait_send()
 
 
-def finish(T, S, hot, units, prob, aux, step, x, up, gain):
+def finish(T, S, onward_too, hot, units, prob, aux, step, x, up, gain):
     tokens, q = x.shape
     shape = jax.ShapeDtypeStruct((tokens, q), bf16)
     dma = pltpu.SemaphoreType.DMA
     return pl.pallas_call(
-        functools.partial(finish_kernel, T, S, q * T),
+        functools.partial(finish_kernel, T, S, q * T, onward_too),
         out_shape=(shape, shape),
         in_specs=vmem(8),
         out_specs=tuple(vmem(2)),
@@ -386,7 +378,7 @@
             pltpu.VMEM((T, tokens, LANES), f32),
             dma((T,)), dma((T,)), dma, dma,
         ],
-        compiler_params=pltpu.CompilerParams(collective_id=2, has_side_effects=True),
+        compiler_params=pltpu.CompilerParams(collective_id=2 if onward_too else 5, has_side_effects=True),
         name="finish",
     )(hot, units, prob, aux, step, x, up, gain)
 
@@ -471,7 +463,7 @@
         prob = jnp.sum(pick(hot_lean, safe) * weight[None, :], axis=-1, keepdims=True)
         prob = jnp.pad(prob, ((0, 0), (0, LANES - 1)))
         result, incoming = finish(
-            T, S, pick(wide_hot, safe), units.reshape(H * cap, q), prob, pick(aux, safe),
+            T, S, S > 1 and tick < micros + S - 2, pick(wide_hot, safe), units.reshape(H * cap, q), prob, pick(aux, safe),
             pick(steps, safe), pick(layer_inputs[0], safe), upstream, gain[None, :],
         )
         updated = lax.dynamic_update_index_in_dim(grads, result, safe, 0)

time: 304 us -> 261 us (0.86)
  Pallas kernels: 268 us -> 226 us
    pallas_call x3, Pallas kernels: 99 us -> 60.9 us  [expert_backward(): pl.pallas_call(functools.partial(experts_kernel, steps), out_shape=(jax.S...]
    pallas_call x3, Pallas kernels: 35.5 us -> 30.8 us  [finish(): pl.pallas_call(functools.partial(finish_kernel, T, S, q * T, onward_too),...]
where the time goes in v2:
time: 261 us
  Pallas kernels  226 us (87%)
  local copies, waits for them, and re-layouts  20 us (8%)
  other arithmetic  10.5 us (4%)
  matrix products  4.05 us (2%)
    pallas_call x3, Pallas kernels, combine(): pl.pallas_call(functools.partial(combine_kernel, H, T, q), out_shape=(jax...  62.9 us
    pallas_call x3, Pallas kernels, expert_backward(): pl.pallas_call(functools.partial(experts_kernel, steps), out_shape=(jax.S...  60.9 us
    pallas_call x3, Pallas kernels, dispatch(): pl.pallas_call(functools.partial(dispatch_kernel, H, group, T, q), out_sh...  60.8 us
    pallas_call x3, Pallas kernels, finish(): pl.pallas_call(functools.partial(finish_kernel, T, S, q * T, onward_too),...  30.8 us
    pallas_call x2, Pallas kernels, tensor_sum(): pl.pallas_call(functools.partial(tensor_sum_kernel, T), out_shape=jax.Sha...  10 us

profile of v2, /device:TPU:0, one launch (start us, length us, event | category | flops | bytes accessed | tf_op | source)
XLA Modules:
  0.0 260.5 jit_solution(12562925463050444086)
XLA Ops:
  1.9 2.4 reduce-window.6
  5.2 1.1 convolution_convert_fusion.2
  6.3 22.1 %dispatch.3 = bf16[4,64,3072]{2,1,0:T(8,128)(2,1)} custom-call(bf16[4,64,768]{2,1,0:T(8,128)(2,1)} %bitcast.150), custom_call_target="tpu_custom_call" | custom-call | tf_op jit(solution)/shard_map/dispatch/pallas_call | solution.py:111
  28.3 20.2 %experts.3 = (bf16[256,3072]{1,0:T(8,128)(2,1)}, f32[256,128]{1,0:T(8,128)}) custom-call(s32[1]{0:T(128)} %bitcast.5.micro_ref, bf16[256,3072]{1,0:T(8,128)(2,1)} %bitcast.141, bf16[2048,3072]{1,0:T(8,128)(2,1)} %bitcast.126, bf16[3072,2048]{1,0:T(8,128)(2,1)} %bitcast.129, bf16[3072,2048]{1,0:T(8,128)(2,1)} %bitcast.132, ...), custom_call_target="tpu_custom_call" | custom-call | tf_op jit(solution)/shard_map/experts/pallas_call | solution.py:167
  48.6 1.1 slice_reduce_fusion.2
  50.4 21.5 %combine.3 = (bf16[4,64,768]{2,1,0:T(8,128)(2,1)}, f32[4,8,128]{2,1,0:T(8,128)}) custom-call(bf16[4,64,3072]{2,1,0:T(8,128)(2,1)} %bitcast.146, f32[4,8,128]{2,1,0:T(8,128)} %pad.37.w_ref), custom_call_target="tpu_custom_call" | custom-call | tf_op jit(solution)/shard_map/combine/pallas_call | solution.py:260
  74.8 5.0 %tensor_sum.2 = f32[8,256]{1,0:T(8,128)} custom-call(f32[8,256]{1,0:T(8,128)} %select_maximum_fusion.3.x_ref), custom_call_target="tpu_custom_call" | custom-call | tf_op jit(solution)/shard_map/tensor_sum/pallas_call | solution.py:308
  80.3 1.4 fusion.37
  82.8 5.0 %tensor_sum.3 = f32[8,256]{1,0:T(8,128)} custom-call(f32[8,256]{1,0:T(8,128)} %pad.40.x_ref), custom_call_target="tpu_custom_call" | custom-call | tf_op jit(solution)/shard_map/tensor_sum/pallas_call | solution.py:308
  94.2 12.2 %finish.3 = (bf16[80,768]{1,0:T(8,128)(2,1)}, bf16[80,768]{1,0:T(8,128)(2,1)}) custom-call(bf16[160,256]{1,0:T(8,128)(2,1)} %get-tuple-element.49.hot_ref, bf16[256,768]{1,0:T(8,128)(2,1)} %bitcast.153, f32[80,128]{1,0:T(8,128)} %pad.38.prob_ref, f32[80,128]{1,0:T(8,128)} %bitcast.156, f32[80,768]{1,0:T(8,128)} %get-tuple-element.43.step_ref, ...), custom_call_target="tpu_custom_call" | custom-call | tf_op jit(solution)/shard_map/finish/pallas_call | solution.py:371
  106.4 0.9 bitcast_select_fusion.3.up_ref
  107.3 1.1 convolution_convert_fusion.1
  108.4 19.4 %dispatch.4 = bf16[4,64,3072]{2,1,0:T(8,128)(2,1)} custom-call(bf16[4,64,768]{2,1,0:T(8,128)(2,1)} %bitcast.151), custom_call_target="tpu_custom_call" | custom-call | tf_op jit(solution)/shard_map/dispatch/pallas_call | solution.py:111
  127.8 20.3 %experts.4 = (bf16[256,3072]{1,0:T(8,128)(2,1)}, f32[256,128]{1,0:T(8,128)}) custom-call(s32[1]{0:T(128)} %bitcast.35.micro_ref, bf16[256,3072]{1,0:T(8,128)(2,1)} %bitcast.142, bf16[2048,3072]{1,0:T(8,128)(2,1)} %bitcast.127, bf16[3072,2048]{1,0:T(8,128)(2,1)} %bitcast.130, bf16[3072,2048]{1,0:T(8,128)(2,1)} %bitcast.133, ...), custom_call_target="tpu_custom_call" | custom-call | tf_op jit(solution)/shard_map/experts/pallas_call | solution.py:167
  148.0 1.0 slice_reduce_fusion.1
  149.7 20.7 %combine.4 = (bf16[4,64,768]{2,1,0:T(8,128)(2,1)}, f32[4,8,128]{2,1,0:T(8,128)}) custom-call(bf16[4,64,3072]{2,1,0:T(8,128)(2,1)} %bitcast.147, f32[4,8,128]{2,1,0:T(8,128)} %pad.42.w_ref), custom_call_target="tpu_custom_call" | custom-call | tf_op jit(solution)/shard_map/combine/pallas_call | solution.py:260
  172.8 11.7 %finish.4 = (bf16[80,768]{1,0:T(8,128)(2,1)}, bf16[80,768]{1,0:T(8,128)(2,1)}) custom-call(bf16[160,256]{1,0:T(8,128)(2,1)} %get-tuple-element.48.hot_ref, bf16[256,768]{1,0:T(8,128)(2,1)} %bitcast.155, f32[80,128]{1,0:T(8,128)} %pad.43.prob_ref, f32[80,128]{1,0:T(8,128)} %bitcast.158, f32[80,768]{1,0:T(8,128)} %get-tuple-element.42.step_ref, ...), custom_call_target="tpu_custom_call" | custom-call | tf_op jit(solution)/shard_map/finish/pallas_call | solution.py:371
  185.5 1.1 convolution_convert_fusion
  186.5 19.4 %dispatch.5 = bf16[4,64,3072]{2,1,0:T(8,128)(2,1)} custom-call(bf16[4,64,768]{2,1,0:T(8,128)(2,1)} %bitcast.149), custom_call_target="tpu_custom_call" | custom-call | tf_op jit(solution)/shard_map/dispatch/pallas_call | solution.py:111
  205.9 20.4 %experts.5 = (bf16[256,3072]{1,0:T(8,128)(2,1)}, f32[256,128]{1,0:T(8,128)}) custom-call(s32[1]{0:T(128)} %bitcast.51.micro_ref, bf16[256,3072]{1,0:T(8,128)(2,1)} %bitcast.143, bf16[2048,3072]{1,0:T(8,128)(2,1)} %bitcast.128, bf16[3072,2048]{1,0:T(8,128)(2,1)} %bitcast.131, bf16[3072,2048]{1,0:T(8,128)(2,1)} %bitcast.134, ...), custom_call_target="tpu_custom_call" | custom-call | tf_op jit(solution)/shard_map/experts/pallas_call | solution.py:167
  226.3 1.0 slice_reduce_fusion
  228.0 20.7 %combine.5 = (bf16[4,64,768]{2,1,0:T(8,128)(2,1)}, f32[4,8,128]{2,1,0:T(8,128)}) custom-call(bf16[4,64,3072]{2,1,0:T(8,128)(2,1)} %bitcast.148, f32[4,8,128]{2,1,0:T(8,128)} %pad.44.w_ref), custom_call_target="tpu_custom_call" | custom-call | tf_op jit(solution)/shard_map/combine/pallas_call | solution.py:260
  251.2 6.9 %finish.5 = (bf16[80,768]{1,0:T(8,128)(2,1)}, bf16[80,768]{1,0:T(8,128)(2,1)}) custom-call(bf16[160,256]{1,0:T(8,128)(2,1)} %get-tuple-element.47.hot_ref, bf16[256,768]{1,0:T(8,128)(2,1)} %bitcast.154, f32[80,128]{1,0:T(8,128)} %pad.45.prob_ref, f32[80,128]{1,0:T(8,128)} %bitcast.157, f32[80,768]{1,0:T(8,128)} %get-tuple-element.41.step_ref, ...), custom_call_target="tpu_custom_call" | custom-call | tf_op jit(solution)/shard_map/finish/pallas_call | solution.py:371
  258.9 1.6 bitcast_dynamic-update-slice_fusion
  (98 shorter events, 22.1 us)
Async XLA Ops:
  0.9 27.4 %copy-start.1 = (bf16[80,768]{1,0:T(8,128)(2,1)}, bf16[80,768]{1,0:T(8,128)(2,1)S(1)}, u32[]{:S(2)}) copy-start(bf16[80,768]{1,0:T(8,128)(2,1)S(1)} %select_bitcast_fusion.up_ref) | copy-start | bytes 368644
  48.6 25.0 %copy-start.8 = (bf16[1,768]{1,0:T(2,128)(2,1)S(1)}, bf16[1,768]{1,0:T(2,128)(2,1)}, u32[]{:S(2)}) copy-start(bf16[1,768]{1,0:T(2,128)(2,1)} %param.12) | copy-start | bytes 4612
  48.6 25.0 %copy-start = (bf16[1,2,80,768]{3,2,1,0:T(8,128)(2,1)S(1)}, bf16[1,2,80,768]{3,2,1,0:T(8,128)(2,1)}, u32[]{:S(2)}) copy-start(bf16[1,2,80,768]{3,2,1,0:T(8,128)(2,1)} %param.10) | copy-start | bytes 737284
  48.6 25.0 %copy-start.7 = (bf16[1,768,4]{1,2,0:T(4,128)(2,1)S(1)}, bf16[1,768,4]{1,2,0:T(4,128)(2,1)}, u32[]{:S(2)}) copy-start(bf16[1,768,4]{1,2,0:T(4,128)(2,1)} %param.13) | copy-start | bytes 18436
  91.9 14.5 %copy-start.4 = (bf16[2,80,768]{2,1,0:T(8,128)(2,1)S(1)}, bf16[2,80,768]{2,1,0:T(8,128)(2,1)}, u32[]{:S(2)}) copy-start(bf16[2,80,768]{2,1,0:T(8,128)(2,1)} %param.11) | copy-start | bytes 737284
  107.3 40.7 %copy-start.3 = (bf16[80,768]{1,0:T(8,128)(2,1)}, bf16[80,768]{1,0:T(8,128)(2,1)S(1)}, u32[]{:S(2)}) copy-start(bf16[80,768]{1,0:T(8,128)(2,1)S(1)} %bitcast_select_fusion.3.up_ref) | copy-start | bytes 368644
  185.4 40.9 %copy-start.2 = (bf16[80,768]{1,0:T(8,128)(2,1)}, bf16[80,768]{1,0:T(8,128)(2,1)S(1)}, u32[]{:S(2)}) copy-start(bf16[80,768]{1,0:T(8,128)(2,1)S(1)} %bitcast_select_fusion.1.up_ref) | copy-start | bytes 368644
  228.0 30.1 %copy-start.5 = (bf16[80,768]{1,0:T(8,128)(2,1)S(1)}, bf16[80,768]{1,0:T(8,128)(2,1)}, u32[]{:S(2)}) copy-start(bf16[80,768]{1,0:T(8,128)(2,1)} %get-tuple-element.26) | copy-start | bytes 368644
  228.0 30.2 %copy-start.6 = (bf16[80,768]{1,0:T(8,128)(2,1)S(1)}, bf16[80,768]{1,0:T(8,128)(2,1)}, u32[]{:S(2)}) copy-start(bf16[80,768]{1,0:T(8,128)(2,1)} %get-tuple-element.32) | copy-start | bytes 368644
